TPU v7x, 32 devices: a whole 2x2x4 slice. The times are simulated.
32 devices in a mesh: groups: 2 (over x), seq: 8 (over z, y), mp: 2 (over core).
Axes of the slice: x: 2, y: 2, z: 4, core: 2. Of those that a mesh axis runs over, the one named last changes fastest.
Arguments:
- latent_cache: bfloat16 [2048, 64, 512], P(('groups', 'seq')), parts along dimension 0, may hold values from -6 to 6
- rope_cache: bfloat16 [2048, 4096], P(('groups', 'seq')), parts along dimension 0, may hold values from -6 to 6
- q_nope: bfloat16 [16, 128, 128], P('groups', 'mp'), parts along dimension 0, may hold values from -12 to 12
- q_rope: bfloat16 [16, 128, 64], P('groups', 'mp'), parts along dimension 0, may hold values from -2000 to 2000
- w_uk: bfloat16 [128, 128, 512], P('mp', None, 'seq'), may hold values from -0.5 to 0.5
- value_up_weight: bfloat16 [128, 512, 128], P('mp', 'seq'), may hold values from -0.25 to 0.25
- w_out: bfloat16 [16384, 7168], P('mp', 'seq'), may hold values from -0.046875 to 0.046875
- page_table: int32 [16, 256], P('groups'), parts along dimension 0, may hold values from 0 to 1023, as said below
- lengths: int32 [16], P('groups'), parts along dimension 0, may hold values from 2048 to 16384, as said below
Outputs:
- output: bfloat16 [16, 7168], P('groups', ('seq', 'mp')), parts along dimension 0
There are 2 independent parts, one for each index of `groups`. A program takes and returns all parts, laid end to end along the dimension named above; an argument that names none is the same for every part. Nothing has to cross between parts.
Inputs may be any that keep to these rules, and one draw needn't show every extreme that they name: `lengths`: every sequence has one eighth of 16384 tokens or more; the longest has exactly 16384. page_table[b,p] for p < ceil(lengths[b] / 64) is the global slot (shard index times 128 plus local slot) holding that page; these live entries are all distinct; the other entries are 0 and unused.
All inputs are finite; a program needn't handle non-finite values.
Results may differ from a plain program's by a relative error of at most 0.012.
Values may be sent and summed in bfloat16 or wider, within the bound.
A program may use at most 128 MiB of HBM per device.

v0:
```python
import jax
import jax.numpy as jnp
from jax import lax
from jax.sharding import PartitionSpec as P

NEG = -1e30


def local(
    latent_cache, rope_cache, q_nope, q_rope, w_uk, value_up_weight, w_out, page_table, lengths
):
    peak_score = lax.Precision.HIGHEST
    slots_dev, page_len, latent_width = latent_cache.shape
    rope_width = q_rope.shape[2]
    seq_count, heads = (q_nope.shape[0], q_nope.shape[1])
    score_scale = (q_nope.shape[2] + rope_width) ** (-0.5)
    q_part = jnp.einsum("bhn,hnk->bhk", q_nope, w_uk, preferred_element_type=jnp.float32).astype(
        jnp.bfloat16
    )
    q_latent = lax.all_gather(q_part, "seq", axis=2, tiled=True)
    first_slot = lax.axis_index("seq") * slots_dev
    page_count = (lengths + page_len - 1) // page_len
    logical = jnp.arange(page_table.shape[1], dtype=jnp.int32)
    live_page = logical[None, :] < page_count[:, None]
    tokens_in = jnp.clip(lengths[:, None] - page_len * logical[None, :], 0, page_len)
    local_ids = jnp.arange(slots_dev, dtype=jnp.int32)
    hits = ((page_table - first_slot)[:, :, None] == local_ids[None, None, :]) & live_page[
        :, :, None
    ]
    owner_mask = jnp.any(hits, axis=1)
    slot_fill = jnp.sum(jnp.where(hits, tokens_in[:, :, None], 0), axis=(0, 1))
    owner_half = owner_mask.astype(jnp.bfloat16)

    def update(run_state, index):
        run_max, run_sum, run_out = run_state
        start = index * 8
        latent_block = lax.dynamic_slice_in_dim(latent_cache, start, 8, 0)
        rope_block = lax.dynamic_slice_in_dim(rope_cache, start, 8, 0).reshape(
            8, page_len, rope_width
        )
        owner_block = lax.dynamic_slice_in_dim(owner_half, start, 8, 1)
        fill_block = lax.dynamic_slice_in_dim(slot_fill, start, 8, 0)
        pick_latent = jnp.einsum(
            "bs,bhk->shk", owner_block, q_latent, preferred_element_type=jnp.float32
        ).astype(jnp.bfloat16)
        pick_rope = jnp.einsum(
            "bs,bhr->shr", owner_block, q_rope, preferred_element_type=jnp.float32
        ).astype(jnp.bfloat16)
        scores = (
            jnp.einsum(
                "shk,stk->sht", pick_latent, latent_block, preferred_element_type=jnp.float32
            )
            + jnp.einsum("shr,str->sht", pick_rope, rope_block, preferred_element_type=jnp.float32)
        ) * score_scale
        live_token = (
            jnp.arange(page_len, dtype=jnp.int32)[None, None, :] < fill_block[:, None, None]
        )
        slot_max = jnp.max(jnp.where(live_token, scores, NEG), axis=2)
        exponent = jnp.where(live_token, jnp.exp(scores - slot_max[:, :, None]), 0.0)
        slot_sum = jnp.sum(exponent, axis=2)
        slot_out = jnp.einsum(
            "sht,stk->shk",
            exponent.astype(jnp.bfloat16),
            latent_block,
            preferred_element_type=jnp.float32,
        )
        owned = owner_block > 0
        candidate = jnp.where(owned[:, :, None], slot_max[None, :, :], NEG)
        new_max = jnp.maximum(run_max, jnp.max(candidate, axis=1))
        carry_scale = jnp.exp(run_max - new_max)
        factor = jnp.where(owned[:, :, None], jnp.exp(candidate - new_max[:, None, :]), 0.0)
        run_sum = run_sum * carry_scale + jnp.einsum(
            "bsh,sh->bh", factor, slot_sum, precision=peak_score
        )
        run_out = run_out * carry_scale[:, :, None] + jnp.einsum(
            "bsh,shk->bhk", factor, slot_out, precision=peak_score
        )
        return (new_max, run_sum, run_out)

    def visit(index, run_state):
        return update(run_state, index)

    initial = (
        jnp.full((seq_count, heads), NEG, jnp.float32),
        jnp.zeros((seq_count, heads), jnp.float32),
        jnp.zeros((seq_count, heads, latent_width), jnp.float32),
    )
    run_max, run_sum, run_out = lax.fori_loop(0, slots_dev // 8, visit, initial)
    share_width = value_up_weight.shape[1]
    shards = lax.axis_size("seq")
    spread_max = jnp.broadcast_to(run_max[:, :, None], (seq_count, heads, shards))
    spread_sum = jnp.broadcast_to(run_sum[:, :, None], (seq_count, heads, shards))
    peers_max, peers_sum, peers_out = (
        lax.all_to_all(spread_max, "seq", split_axis=2, concat_axis=2, tiled=True),
        lax.all_to_all(spread_sum, "seq", split_axis=2, concat_axis=2, tiled=True),
        lax.all_to_all(run_out, "seq", split_axis=2, concat_axis=2, tiled=True),
    )
    top = jnp.max(peers_max, axis=2)
    rescale = jnp.exp(peers_max - top[:, :, None])
    totals = jnp.sum(peers_sum * rescale, axis=2)
    grouped = peers_out.reshape(seq_count, heads, shards, share_width)
    shared_latent = jnp.sum(grouped * rescale[:, :, :, None], axis=2)
    local_portion = (shared_latent / totals[:, :, None]).astype(jnp.bfloat16)
    value_slice = jnp.einsum(
        "gre,req->grq", local_portion, value_up_weight, preferred_element_type=jnp.float32
    )
    value_rows = lax.psum(value_slice, "seq").astype(jnp.bfloat16)
    flat_values = value_rows.reshape(seq_count, heads * value_rows.shape[2])
    partial_out = jnp.dot(flat_values, w_out, preferred_element_type=jnp.float32)
    return lax.psum_scatter(partial_out, "mp", scatter_dimension=1, tiled=True).astype(jnp.bfloat16)


def solution(mesh):
    return jax.shard_map(
        local,
        mesh=mesh,
        in_specs=(
            P(("groups", "seq"), None, None),
            P(("groups", "seq"), None),
            P("groups", "mp", None),
            P("groups", "mp", None),
            P("mp", None, "seq"),
            P("mp", "seq", None),
            P("mp", "seq"),
            P("groups", None),
            P("groups"),
        ),
        out_specs=P("groups", ("seq", "mp")),
        check_vma=False,
    )
```

profile of v0, /device:TPU:0, one launch (start us, length us, event | category | flops | bytes accessed | tf_op | source)
XLA Modules:
  0.0 317.1 jit_solution(13368818275387407663)
XLA Ops:
  10.1 1.9 fusion.40
  13.1 36.4 %all_gather.3 = bf16[8,64,512]{1,0,2:T(8,128)(2,1)} all-gather(bf16[8,64,64]{1,0,2:T(8,128)(2,1)S(1)} %copy.63), channel_id=1, replica_groups=mesh['groups'=2,'seq'=8,'mp'=2] {'seq'}, dimensions={2}, use_global_device_ids=true | all-gather | bytes 589824 | tf_op jit(solution)/shard_map/all_gather | solution.py:20
  49.6 2.3 copy.65
  51.9 129.9 %while.18 = (s32[]{:T(128)}, f32[8,64]{0,1:T(8,128)S(1)}, f32[8,64]{0,1:T(8,128)S(1)}, f32[8,64,512]{2,0,1:T(8,128)S(1)}, bf16[8,128]{1,0:T(8,128)(2,1)S(1)}, /*...) while((s32[]{:T(128)}, f32[8,64]{0,1:T(8,128)S(1)}, ...), condition=%wide.region_6.7_spmd.clone, body=%wide.region_2.6_spmd.clone.sunk | while | flops 102681152 | bytes 8056379 | solution.py:88
  56.7 1.5 fusion.90
  58.2 1.8 fusion.91
  62.0 1.4 fusion.86
  64.8 1.5 fusion.90
  66.3 1.8 fusion.91
  70.2 1.4 fusion.86
  72.9 1.5 fusion.90
  74.5 1.8 fusion.91
  78.3 1.4 fusion.86
  81.0 1.5 fusion.90
  82.6 1.8 fusion.91
  86.4 1.4 fusion.86
  89.2 1.5 fusion.90
  90.7 1.8 fusion.91
  94.5 1.4 fusion.86
  97.3 1.5 fusion.90
  98.8 1.8 fusion.91
  102.6 1.4 fusion.86
  105.4 1.5 fusion.90
  106.9 1.8 fusion.91
  110.7 1.4 fusion.86
  113.5 1.5 fusion.90
  115.0 1.8 fusion.91
  118.9 1.4 fusion.86
  121.6 1.5 fusion.90
  123.2 1.8 fusion.91
  127.0 1.4 fusion.86
  129.8 1.5 fusion.90
  131.3 1.8 fusion.91
  135.1 1.4 fusion.86
  137.9 1.5 fusion.90
  139.4 1.8 fusion.91
  143.2 1.4 fusion.86
  146.0 1.5 fusion.90
  147.5 1.8 fusion.91
  154.1 1.5 fusion.90
  155.6 1.8 fusion.91
  159.5 1.4 fusion.86
  162.2 1.5 fusion.90
  163.7 1.8 fusion.91
  170.3 1.5 fusion.90
  171.9 1.8 fusion.91
  178.5 1.5 fusion.90
  180.0 1.8 fusion.91
  182.5 5.3 %all-to-all-start.2 = ((f32[8,1,512]{2,1,0:T(1,128)}), f32[8,1,512]{2,1,0:T(1,128)S(1)}, u32[]{:S(2)}, u32[]{:S(2)}) async-start(f32[8,1,512]{2,1,0:T(1,128)} %reshape.112), calls=%async_computation.2 | async-start | bytes 32768 | tf_op jit(solution)/shard_map/all_to_all | solution.py:95
  188.6 5.8 %all-to-all-done.2 = f32[8,1,512]{2,1,0:T(1,128)S(1)} async-done(((f32[8,1,512]{2,1,0:T(1,128)}), f32[8,1,512]{2,1,0:T(1,128)S(1)}, u32[]{:S(2)}, u32[]{:S(2)}) %all-to-all-start.2) | async-done | bytes 16416 | tf_op jit(solution)/shard_map/all_to_all | solution.py:95
  194.4 3.3 %all-to-all-start.1 = ((f32[8,1,512]{2,1,0:T(1,128)}), f32[8,1,512]{2,1,0:T(1,128)S(1)}, u32[]{:S(2)}, u32[]{:S(2)}) async-start(f32[8,1,512]{2,1,0:T(1,128)} %reshape.110), calls=%async_computation.1 | async-start | bytes 32768 | tf_op jit(solution)/shard_map/all_to_all | solution.py:94
  197.8 2.3 copy.67
  200.1 3.4 %reshape.108 = f32[8,1,32768]{2,1,0:T(1,128)} reshape(f32[512,8,64]{2,1,0:T(8,128)} %bitcast.64) | data formatting | bytes 2097152
  204.4 5.0 %all-to-all-start = ((f32[8,1,32768]{2,1,0:T(1,128)}), f32[8,1,32768]{2,1,0:T(1,128)S(1)}, u32[]{:S(2)}, u32[]{:S(2)}) async-start(f32[8,1,32768]{2,1,0:T(1,128)} %reshape.108), calls=%async_computation | async-start | bytes 2097152 | tf_op jit(solution)/shard_map/all_to_all | solution.py:96
  211.9 16.0 %all-to-all-done = f32[8,1,32768]{2,1,0:T(1,128)S(1)} async-done(((f32[8,1,32768]{2,1,0:T(1,128)}), f32[8,1,32768]{2,1,0:T(1,128)S(1)}, u32[]{:S(2)}, u32[]{:S(2)}) %all-to-all-start) | async-done | bytes 1048608 | tf_op jit(solution)/shard_map/all_to_all | solution.py:96
  227.9 3.1 reduce
  231.0 2.2 reshape.109
  233.2 9.4 %copy.70 = f32[8,64,8,64]{0,1,3,2:T(8,128)} copy(f32[8,64,8,64]{1,0,3,2:T(8,128)} %bitcast.63) | data formatting | bytes 2097152 | tf_op jit(solution)/shard_map/reshape | solution.py:101
  242.6 9.7 %multiply_reduce_fusion = f32[8,64,64]{0,1,2:T(8,128)} fusion(f32[8,64,8,64]{0,1,3,2:T(8,128)} %copy.70, f32[8,64,8]{0,1,2:T(8,128)S(1)} %copy.69), kind=kLoop, calls=%fused_computation.53 | loop fusion | flops 491520 | bytes 1196032 | tf_op jit(solution)/shard_map/reduce_sum | solution.py:102
  252.3 2.7 copy.72
  255.5 38.2 %all-reduce.1 = bf16[8,64,128]{2,0,1:T(8,128)(2,1)S(1)} all-reduce(f32[8,64,128]{2,0,1:T(8,128)S(1)} %convolution_bitcast_fusion.2), channel_id=1, replica_groups=mesh['groups'=2,'seq'=8,'mp'=2] {'seq'}, use_global_device_ids=true, to_apply=%region_10.11 | all-reduce | flops 65536 | bytes 393216 | tf_op jit(solution)/shard_map/psum | solution.py:107
  293.8 9.8 %convolution_bitcast_fusion.1 = f32[896,8]{1,0:T(8,128)} fusion(bf16[8192,896]{1,0:T(8,128)(2,1)} %param.17, bf16[8,64,128]{2,0,1:T(8,128)(2,1)S(1)} %all-reduce.1), kind=kOutput, calls=%fused_computation.54 | convolution fusion | flops 117440512 | bytes 14839808
  303.6 5.1 %reduce-scatter.4.cloned.1.call-done = f32[448,8]{1,0:T(8,128)} async-done(((f32[896,8]{1,0:T(8,128)}), f32[448,8]{1,0:T(8,128)}) %reduce-scatter.4.cloned.1.call-update) | async-done | bytes 14352
  308.6 1.6 copy.78
  (341 shorter events, 69.2 us)
Async XLA Ops:
  6.5 248.6 %copy-start = (bf16[64,64,128]{2,1,0:T(8,128)(2,1)S(1)}, bf16[64,64,128]{2,1,0:T(8,128)(2,1)}, u32[]{:S(2)}) copy-start(bf16[64,64,128]{2,1,0:T(8,128)(2,1)} %param.16) | copy-start | bytes 3145732
  182.5 11.9 %all-to-all-start.2 = ((f32[8,1,512]{2,1,0:T(1,128)}), f32[8,1,512]{2,1,0:T(1,128)S(1)}, u32[]{:S(2)}, u32[]{:S(2)}) async-start(f32[8,1,512]{2,1,0:T(1,128)} %reshape.112), calls=%async_computation.2 | async-start | bytes 32768 | tf_op jit(solution)/shard_map/all_to_all | solution.py:95
  194.4 9.9 %all-to-all-start.1 = ((f32[8,1,512]{2,1,0:T(1,128)}), f32[8,1,512]{2,1,0:T(1,128)S(1)}, u32[]{:S(2)}, u32[]{:S(2)}) async-start(f32[8,1,512]{2,1,0:T(1,128)} %reshape.110), calls=%async_computation.1 | async-start | bytes 32768 | tf_op jit(solution)/shard_map/all_to_all | solution.py:94
  204.4 23.5 %all-to-all-start = ((f32[8,1,32768]{2,1,0:T(1,128)}), f32[8,1,32768]{2,1,0:T(1,128)S(1)}, u32[]{:S(2)}, u32[]{:S(2)}) async-start(f32[8,1,32768]{2,1,0:T(1,128)} %reshape.108), calls=%async_computation | async-start | bytes 2097152 | tf_op jit(solution)/shard_map/all_to_all | solution.py:96
  209.4 99.2 %reduce-scatter.4.cloned.1.call-start = ((), (), s32[]{:S(2)}) async-start(), calls=%async_computation.4 | async-start | bytes 688128
Sparse Core Ops, SparseCore 0:
  303.7 4.9 reduce-scatter.3
where the time goes:
time: 320 us; the launch traced here: 317 us
  matrix products  110 us (34%)
  blocking collectives  74.7 us (23%)
  local copies, waits for them, and re-layouts  51.6 us (16%)
  waiting for transfers between devices  27.9 us (9%)
  other arithmetic  24.3 us (8%)
  starting transfers between devices  13.9 us (4%)
  between operations  13.5 us (4%)
    psum x1, blocking collectives, local(): value_rows = lax.psum(value_slice, 'seq').astype(jnp.bfloat16)  38.2 us
    all_gather x1, blocking collectives, local(): q_latent = lax.all_gather(q_part, 'seq', axis=2, tiled=True)  36.4 us
    dot_general x16, matrix products, update(): jnp.einsum('bsh,shk->bhk', factor, slot_out, precision=peak_score)  28.3 us
    dot_general x16, matrix products, update(): jnp.einsum('sht,stk->shk', exponent.astype(jnp.bfloat16), latent_block, p...  24.3 us
    dot_general x16, matrix products, update(): jnp.einsum('shk,stk->sht', pick_latent, latent_block, preferred_element_t...  22 us
    all_to_all x1, waiting for transfers between devices, local(): lax.all_to_all(run_out, 'seq', split_axis=2, concat_axis=2, tiled=True)  16 us
    dynamic_slice x16, local copies, waits for them, and re-layouts, update(): lax.dynamic_slice_in_dim(rope_cache, start, 8, 0)  13.5 us
    unnamed x13, local copies, waits for them, and re-layouts  12 us
  transfers between devices with their start and end apart: 4, of which 4 were waited for; matrix products, arithmetic and copies ran while one was open for 3% of the time, Pallas kernels for 0%

commit v1 on v0

--- a/solution.py
+++ b/solution.py
@@ -104,7 +104,7 @@
     value_slice = jnp.einsum(
         "gre,req->grq", local_portion, value_up_weight, preferred_element_type=jnp.float32
     )
-    value_rows = lax.psum(value_slice, "seq").astype(jnp.bfloat16)
+    value_rows = jnp.sum(lax.all_gather(value_slice, "seq"), axis=0).astype(jnp.bfloat16)
     flat_values = value_rows.reshape(seq_count, heads * value_rows.shape[2])
     partial_out = jnp.dot(flat_values, w_out, preferred_element_type=jnp.float32)
     return lax.psum_scatter(partial_out, "mp", scatter_dimension=1, tiled=True).astype(jnp.bfloat16)

time: 320 us -> 335 us (1.047)
  waiting for transfers between devices: 27.9 us -> 78.3 us
  blocking collectives: 74.7 us -> 36.4 us
    all_gather x0 -> x1, waiting for transfers between devices: none -> 49.3 us  [local(): lax.all_gather(value_slice, 'seq')]
    psum x1 -> x0, blocking collectives: 38.2 us -> none  [local(): value_rows = lax.psum(value_slice, 'seq').astype(jnp.bfloat16)]
  transfers between devices with their start and end apart: 4 -> 5, of which waited for: 4 -> 5; matrix products, arithmetic and copies ran while one was open for 3% -> 3% of each run, Pallas kernels for 0% -> 0%
where the time goes in v1:
time: 335 us; the launch traced here: 332 us
  matrix products  110 us (33%)
  waiting for transfers between devices  78.3 us (23%)
  local copies, waits for them, and re-layouts  51.6 us (15%)
  blocking collectives  36.4 us (11%)
  other arithmetic  26.1 us (8%)
  starting transfers between devices  13.9 us (4%)
  between operations  13.5 us (4%)
    all_gather x1, waiting for transfers between devices, local(): lax.all_gather(value_slice, 'seq')  49.3 us
    all_gather x1, blocking collectives, local(): q_latent = lax.all_gather(q_part, 'seq', axis=2, tiled=True)  36.4 us
    dot_general x16, matrix products, update(): jnp.einsum('bsh,shk->bhk', factor, slot_out, precision=peak_score)  28.3 us
    dot_general x16, matrix products, update(): jnp.einsum('sht,stk->shk', exponent.astype(jnp.bfloat16), latent_block, p...  24.3 us
    dot_general x16, matrix products, update(): jnp.einsum('shk,stk->sht', pick_latent, latent_block, preferred_element_t...  22 us
    all_to_all x1, waiting for transfers between devices, local(): lax.all_to_all(run_out, 'seq', split_axis=2, concat_axis=2, tiled=True)  16 us
    dynamic_slice x16, local copies, waits for them, and re-layouts, update(): lax.dynamic_slice_in_dim(rope_cache, start, 8, 0)  13.5 us
    unnamed x13, local copies, waits for them, and re-layouts  12 us
  transfers between devices with their start and end apart: 5, of which 5 were waited for; matrix products, arithmetic and copies ran while one was open for 3% of the time, Pallas kernels for 0%

profile of v1, /device:TPU:0, one launch (start us, length us, event | category | flops | bytes accessed | tf_op | source)
XLA Modules:
  0.0 331.9 jit_solution(12469515393131110391)
XLA Ops:
  10.1 1.9 fusion.40
  13.1 36.4 %all_gather.9 = bf16[8,64,512]{1,0,2:T(8,128)(2,1)} all-gather(bf16[8,64,64]{1,0,2:T(8,128)(2,1)S(1)} %copy.63), channel_id=1, replica_groups=mesh['groups'=2,'seq'=8,'mp'=2] {'seq'}, dimensions={2}, use_global_device_ids=true | all-gather | bytes 589824 | tf_op jit(solution)/shard_map/all_gather | solution.py:20
  49.6 2.3 copy.65
  51.9 129.9 %while.18 = (s32[]{:T(128)}, f32[8,64]{0,1:T(8,128)S(1)}, f32[8,64]{0,1:T(8,128)S(1)}, f32[8,64,512]{2,0,1:T(8,128)S(1)}, bf16[8,128]{1,0:T(8,128)(2,1)S(1)}, /*...) while((s32[]{:T(128)}, f32[8,64]{0,1:T(8,128)S(1)}, ...), condition=%wide.region_6.7_spmd.clone, body=%wide.region_2.6_spmd.clone.sunk | while | flops 102681152 | bytes 8056379 | solution.py:88
  56.7 1.5 fusion.90
  58.2 1.8 fusion.91
  62.0 1.4 fusion.86
  64.8 1.5 fusion.90
  66.3 1.8 fusion.91
  70.2 1.4 fusion.86
  72.9 1.5 fusion.90
  74.5 1.8 fusion.91
  78.3 1.4 fusion.86
  81.0 1.5 fusion.90
  82.6 1.8 fusion.91
  86.4 1.4 fusion.86
  89.2 1.5 fusion.90
  90.7 1.8 fusion.91
  94.5 1.4 fusion.86
  97.3 1.5 fusion.90
  98.8 1.8 fusion.91
  102.6 1.4 fusion.86
  105.4 1.5 fusion.90
  106.9 1.8 fusion.91
  110.7 1.4 fusion.86
  113.5 1.5 fusion.90
  115.0 1.8 fusion.91
  118.9 1.4 fusion.86
  121.6 1.5 fusion.90
  123.2 1.8 fusion.91
  127.0 1.4 fusion.86
  129.8 1.5 fusion.90
  131.3 1.8 fusion.91
  135.1 1.4 fusion.86
  137.9 1.5 fusion.90
  139.4 1.8 fusion.91
  146.0 1.5 fusion.90
  147.5 1.8 fusion.91
  154.1 1.5 fusion.90
  155.6 1.8 fusion.91
  159.5 1.4 fusion.86
  162.2 1.5 fusion.90
  163.7 1.8 fusion.91
  170.3 1.5 fusion.90
  171.9 1.8 fusion.91
  178.5 1.5 fusion.90
  180.0 1.8 fusion.91
  182.5 5.3 %all-to-all-start.2 = ((f32[8,1,512]{2,1,0:T(1,128)}), f32[8,1,512]{2,1,0:T(1,128)S(1)}, u32[]{:S(2)}, u32[]{:S(2)}) async-start(f32[8,1,512]{2,1,0:T(1,128)} %reshape.112), calls=%async_computation.2 | async-start | bytes 32768 | tf_op jit(solution)/shard_map/all_to_all | solution.py:95
  188.6 5.8 %all-to-all-done.2 = f32[8,1,512]{2,1,0:T(1,128)S(1)} async-done(((f32[8,1,512]{2,1,0:T(1,128)}), f32[8,1,512]{2,1,0:T(1,128)S(1)}, u32[]{:S(2)}, u32[]{:S(2)}) %all-to-all-start.2) | async-done | bytes 16416 | tf_op jit(solution)/shard_map/all_to_all | solution.py:95
  194.4 3.3 %all-to-all-start.1 = ((f32[8,1,512]{2,1,0:T(1,128)}), f32[8,1,512]{2,1,0:T(1,128)S(1)}, u32[]{:S(2)}, u32[]{:S(2)}) async-start(f32[8,1,512]{2,1,0:T(1,128)} %reshape.110), calls=%async_computation.1 | async-start | bytes 32768 | tf_op jit(solution)/shard_map/all_to_all | solution.py:94
  197.8 2.3 copy.67
  200.1 3.4 %reshape.108 = f32[8,1,32768]{2,1,0:T(1,128)} reshape(f32[512,8,64]{2,1,0:T(8,128)} %bitcast.66) | data formatting | bytes 2097152
  204.4 5.0 %all-to-all-start = ((f32[8,1,32768]{2,1,0:T(1,128)}), f32[8,1,32768]{2,1,0:T(1,128)S(1)}, u32[]{:S(2)}, u32[]{:S(2)}) async-start(f32[8,1,32768]{2,1,0:T(1,128)} %reshape.108), calls=%async_computation | async-start | bytes 2097152 | tf_op jit(solution)/shard_map/all_to_all | solution.py:96
  211.9 16.0 %all-to-all-done = f32[8,1,32768]{2,1,0:T(1,128)S(1)} async-done(((f32[8,1,32768]{2,1,0:T(1,128)}), f32[8,1,32768]{2,1,0:T(1,128)S(1)}, u32[]{:S(2)}, u32[]{:S(2)}) %all-to-all-start) | async-done | bytes 1048608 | tf_op jit(solution)/shard_map/all_to_all | solution.py:96
  227.9 3.1 reduce
  231.0 2.2 reshape.109
  233.2 9.4 %copy.70 = f32[8,64,8,64]{0,1,3,2:T(8,128)} copy(f32[8,64,8,64]{1,0,3,2:T(8,128)} %bitcast.65) | data formatting | bytes 2097152 | tf_op jit(solution)/shard_map/reshape | solution.py:101
  242.6 9.7 %multiply_reduce_fusion = f32[8,64,64]{0,1,2:T(8,128)} fusion(f32[8,64,8,64]{0,1,3,2:T(8,128)} %copy.70, f32[8,64,8]{0,1,2:T(8,128)S(1)} %copy.69), kind=kLoop, calls=%fused_computation.53 | loop fusion | flops 491520 | bytes 1196032 | tf_op jit(solution)/shard_map/reduce_sum | solution.py:102
  252.3 2.7 copy.72
  256.3 49.3 %all-gather.3.cloned.1.call-done = f32[64,64,128]{2,0,1:T(8,128)} async-done(((f32[8,64,128]{2,0,1:T(8,128)}), f32[64,64,128]{2,0,1:T(8,128)}) %all-gather.3.cloned.1.call-update) | async-done | bytes 2097168 | tf_op jit(solution)/shard_map/all_gather | solution.py:107
  305.7 1.8 bitcast_reduce_fusion
  307.5 9.8 %convolution_bitcast_fusion.1 = f32[896,8]{1,0:T(8,128)} fusion(bf16[8192,896]{1,0:T(8,128)(2,1)} %param.17, bf16[8,64,128]{2,0,1:T(8,128)(2,1)S(1)} %bitcast_reduce_fusion), kind=kOutput, calls=%fused_computation.55 | convolution fusion | flops 117440512 | bytes 14839808
  317.3 6.2 %reduce-scatter.4.cloned.1.call-done = f32[448,8]{1,0:T(8,128)} async-done(((f32[896,8]{1,0:T(8,128)}), f32[448,8]{1,0:T(8,128)}) %reduce-scatter.4.cloned.1.call-update) | async-done | bytes 14352
  323.5 1.6 copy.78
  (344 shorter events, 71.4 us)
Async XLA Ops:
  6.5 248.6 %copy-start = (bf16[64,64,128]{2,1,0:T(8,128)(2,1)S(1)}, bf16[64,64,128]{2,1,0:T(8,128)(2,1)}, u32[]{:S(2)}) copy-start(bf16[64,64,128]{2,1,0:T(8,128)(2,1)} %param.16) | copy-start | bytes 3145732
  182.5 11.9 %all-to-all-start.2 = ((f32[8,1,512]{2,1,0:T(1,128)}), f32[8,1,512]{2,1,0:T(1,128)S(1)}, u32[]{:S(2)}, u32[]{:S(2)}) async-start(f32[8,1,512]{2,1,0:T(1,128)} %reshape.112), calls=%async_computation.2 | async-start | bytes 32768 | tf_op jit(solution)/shard_map/all_to_all | solution.py:95
  194.4 9.9 %all-to-all-start.1 = ((f32[8,1,512]{2,1,0:T(1,128)}), f32[8,1,512]{2,1,0:T(1,128)S(1)}, u32[]{:S(2)}, u32[]{:S(2)}) async-start(f32[8,1,512]{2,1,0:T(1,128)} %reshape.110), calls=%async_computation.1 | async-start | bytes 32768 | tf_op jit(solution)/shard_map/all_to_all | solution.py:94
  204.4 23.5 %all-to-all-start = ((f32[8,1,32768]{2,1,0:T(1,128)}), f32[8,1,32768]{2,1,0:T(1,128)S(1)}, u32[]{:S(2)}, u32[]{:S(2)}) async-start(f32[8,1,32768]{2,1,0:T(1,128)} %reshape.108), calls=%async_computation | async-start | bytes 2097152 | tf_op jit(solution)/shard_map/all_to_all | solution.py:96
  209.4 96.2 %all-gather.3.cloned.1.call-start = ((), (), s32[]{:S(2)}) async-start(), calls=%async_computation.4 | async-start | bytes 2359296 | tf_op jit(solution)/shard_map/all_gather | solution.py:107
  256.3 67.2 %reduce-scatter.4.cloned.1.call-start = ((), (), s32[]{:S(2)}) async-start(), calls=%async_computation.5 | async-start | bytes 688128
Sparse Core Ops, SparseCore 0:
  256.4 49.2 all-gather.2
  317.4 6.0 reduce-scatter.3
